TPU v7x, 256 devices: a whole 4x4x8 slice. The times are simulated.
256 devices in a mesh: dp: 8 (over x, core), vocab: 32 (over z, y).
Axes of the slice: x: 4, y: 4, z: 8, core: 2. Of those that a mesh axis runs over, the one named last changes fastest.
Arguments:
- hidden: bfloat16 [1024, 8192], P(('dp', 'vocab')), may hold values from -350 to 350
- lm_head: bfloat16 [8192, 128256], P(None, ('dp', 'vocab')), may hold values from -0.0625 to 0.0625
- targets: int32 [1024], P(('dp', 'vocab')), may hold values from 0 to 128255
- segment: int32 [1024], P(('dp', 'vocab')), may hold values from 0 to 256, as said below
- pad_mask: int32 [1024], P(('dp', 'vocab')), may hold values from 0 to 1, as said below
- seq_bench: int32 [257], replicated, may hold values from 0 to 7
Outputs:
- token_nll: float32 [1024], P(('dp', 'vocab'))
- bench_total: float32 [8], replicated
- bench_count: float32 [8], replicated
Inputs may be any that keep to these rules, and one draw needn't show every extreme that they name: `segment`: sequence numbers never fall along the pack; each aligned block of 4 tokens holds exactly one place inside it where the number rises by one, and the number does not change between one block's last token and the next block's first. `pad_mask`: the last token of each aligned block of 4 tokens is real.
All inputs are finite; a program needn't handle non-finite values.
Results may differ from a plain program's by a relative error of at most 0.0003.
Values may be sent and summed in bfloat16 or wider, within the bound.
A program may use at most 128 MiB of HBM per device.

v0:
```python
from functools import partial
import functools
import jax
import jax.numpy as jnp
from jax import lax
from jax.sharding import Mesh
from jax.sharding import PartitionSpec as P

NBENCH = 8
DP_VOCAB = ("dp_0", "dp_1", "vocab_0", "vocab_1")
VOCAB = ("vocab_0", "vocab_1")
DP = ("dp_0", "dp_1")


def laid_out(pieces, dim):
    pieces = jnp.moveaxis(pieces, 0, dim)
    shape = pieces.shape
    return pieces.reshape(*shape[:dim], shape[dim] * shape[dim + 1], *shape[dim + 2 :])


def gather_in_order(value, axes, sequence):
    pieces = value
    for k in sequence:
        pieces = lax.all_gather(pieces, axes[k])
    done = sequence[::-1]
    back = [done.index(k) for k in range(len(axes))]
    pieces = pieces.transpose(*back, *range(len(axes), pieces.ndim))
    return pieces.reshape(-1, *value.shape)


def gathered_by_axis(value, axes, sequence, dim):
    return laid_out(gather_in_order(value, axes, sequence), dim)


def whole_of(value, axes, dim):
    out = value
    for number in range(len(axes) - 1, -1, -1):
        out = lax.all_gather(out, axes[number], axis=dim, tiled=True)
    return out


def gathered_once(value, axis):
    leaves = jax.tree.leaves(value)
    sequence = sorted(range(len(leaves)), key=lambda k: -leaves[k].size)
    width = (1, *leaves[sequence[0]].shape)[-1]
    lines = [
        jnp.pad(leaves[k].reshape(-1), (0, -leaves[k].size % width)).reshape(-1, width)
        for k in sequence
    ]
    both, at, found = (lax.all_gather(jnp.concatenate(lines), axis), 0, {})
    for k, line in zip(sequence, lines):
        share = both[:, at : at + len(line)].reshape(len(both), -1)
        found[k] = share[:, : leaves[k].size].reshape(-1, *leaves[k].shape)
        at += len(line)
    numbers = iter(range(len(leaves)))
    return jax.tree.map(lambda _: found[next(numbers)], value)


def merged_by_axis(value, axes, combine):
    for axis in axes:
        pieces = gathered_once(value, axis)
        value = jax.tree.map(lambda part: part[0], pieces)
        for k in range(1, lax.axis_size(axis)):
            value = combine(value, jax.tree.map(lambda part: part[k], pieces))
    return value


def from_behind(value, axis, steps):
    count = lax.axis_size(axis)
    leading, last = (max(0, -steps), min(count, count - steps))
    return lax.ppermute(value, axis, [(source, source + steps) for source in range(leading, last)])


def one_axis_at_a_time(value, axes):
    return functools.reduce(lax.psum, axes, value)


def shard_stats(piece, start, lm_head, all_targets, col_start):
    logits = jnp.dot(piece, lm_head, preferred_element_type=jnp.float32)
    row_top = jnp.max(logits, axis=1)
    expsum = jnp.sum(jnp.exp(logits - row_top[:, None]), axis=1)
    wanted = all_targets - col_start
    columns = lax.broadcasted_iota(jnp.int32, logits.shape, 1)
    picked = jnp.sum(jnp.where(columns == wanted[:, None], logits, 0.0), axis=1)
    return jnp.stack([row_top, expsum, picked], axis=0)


def merge_rows(first, second):
    top = jnp.maximum(first[0], second[0])
    total = first[1] * jnp.exp(first[0] - top) + second[1] * jnp.exp(second[0] - top)
    return (top, total, first[2] + second[2])


def body(hidden, lm_head, targets, segment, pad_mask, seq_bench):
    tok_dev = hidden.shape[0]
    voc_dev = lm_head.shape[1]
    own_index = lax.axis_index(DP_VOCAB)
    col_start = own_index * voc_dev
    row_start = own_index * tok_dev
    all_targets = gathered_by_axis(targets, DP_VOCAB, (0, 2, 3, 1), 0)
    per_piece = partial(shard_stats, lm_head=lm_head, all_targets=all_targets, col_start=col_start)
    group_rows = whole_of(hidden, VOCAB, 0)
    stats = per_piece(lax.all_gather(group_rows, DP, axis=0, tiled=True), jnp.int32(0))
    top_all, total_all, picked_all = merged_by_axis(
        (stats[0], stats[1], stats[2]), DP_VOCAB, merge_rows
    )
    top = lax.dynamic_slice_in_dim(top_all, row_start, tok_dev, 0)
    total = lax.dynamic_slice_in_dim(total_all, row_start, tok_dev, 0)
    picked = lax.dynamic_slice_in_dim(picked_all, row_start, tok_dev, 0)
    token_nll = top + jnp.log(total) - picked
    next_first = from_behind(segment[:1] + 1, DP_VOCAB, -1)
    following = jnp.concatenate([segment[1:] + 1, next_first])
    keep = (pad_mask * (segment + 1 == following).astype(jnp.int32)).astype(jnp.float32)
    seq_count = seq_bench.shape[0]
    seq_hot = segment[:, None] == lax.broadcasted_iota(jnp.int32, (1, seq_count), 1)
    bench_of = jnp.sum(jnp.where(seq_hot, seq_bench[None, :], 0), axis=1)
    bench_hot = (bench_of[:, None] == lax.broadcasted_iota(jnp.int32, (1, NBENCH), 1)).astype(
        jnp.float32
    )
    weighted = keep * token_nll
    bench_total, bench_count = (
        one_axis_at_a_time(jnp.sum(bench_hot * weighted[:, None], axis=0), DP_VOCAB),
        one_axis_at_a_time(jnp.sum(bench_hot * keep[:, None], axis=0), DP_VOCAB),
    )
    return (token_nll, bench_total, bench_count)


def solution(mesh):
    split = Mesh(mesh.devices.reshape(4, 2, 8, 4), ("dp_0", "dp_1", "vocab_0", "vocab_1"))
    return jax.shard_map(
        body,
        mesh=split,
        in_specs=(P(DP_VOCAB, None), P(None, DP_VOCAB), P(DP_VOCAB), P(DP_VOCAB), P(DP_VOCAB), P()),
        out_specs=(P(DP_VOCAB), P(), P()),
        check_vma=False,
    )
```

profile of v0, /device:TPU:2, one launch (start us, length us, event | category | flops | bytes accessed | tf_op | source)
XLA Modules:
  0.0 264.9 jit_solution(8159874351671681301)
XLA Ops:
  7.3 13.0 %all-gather.8 = bf16[4,4,8192]{2,1,0:T(4,128)(2,1)S(1)} all-gather(bf16[1,4,8192]{2,1,0:T(4,128)(2,1)} %bitcast.295), channel_id=1, replica_groups=mesh['dp_0'=4,'dp_1'=2,'vocab_0'=8,'vocab_1'=4] {'vocab_1'}, dimensions={0}, use_global_device_ids=true | all-gather | bytes 327680 | tf_op jit(solution)/shard_map/all_gather | solution.py:38
  20.2 0.8 reshape.920
  21.0 0.0 all-gather.19.cloned.1.call-start
  21.1 43.2 %all-gather.17.cloned.1.call-done = bf16[128,8192]{1,0:T(8,128)(2,1)} async-done(((bf16[16,8192]{1,0:T(8,128)(2,1)}), bf16[128,8192]{1,0:T(8,128)(2,1)}) %all-gather.17.cloned.1.call-update) | async-done | bytes 2097168 | tf_op jit(solution)/shard_map/all_gather | solution.py:38
  64.4 3.2 %collective-permute-start = (s32[1]{0:T(128)}, s32[1]{0:T(128)}, u32[]{:S(2)}, u32[]{:S(2)}) collective-permute-start(s32[1]{0:T(128)} %add.335), channel_id=1, source_target_pairs={{1,0},{2,1},{3,2},{4,3},{5,4},{6,5},{7,6},{8,7},{9,8},{10,9},{11,1... | collective-permute-start | bytes 20 | tf_op jit(solution)/shard_map/ppermute | solution.py:71
  67.6 0.6 dynamic-slice.1
  68.9 0.2 dynamic-update-slice
  69.1 7.9 %all-reduce = s32[16]{0:T(128)S(1)} all-reduce(s32[16]{0:T(128)S(1)} %dynamic-update-slice), channel_id=2, replica_groups=mesh['dp_0'=4,'dp_1'=2,'vocab_0'=8,'vocab_1'=4] {'dp_0'}, use_global_device_ids=true, to_apply=%add | all-reduce | flops 16 | bytes 128
  77.0 0.1 reshape.921
  77.1 26.0 %all-gather.9 = s32[8,4,4]{2,1,0:T(4,128)S(1)} all-gather(s32[1,4,4]{2,1,0:T(4,128)S(1)} %reshape.921), channel_id=3, replica_groups=mesh['dp_0'=4,'dp_1'=2,'vocab_0'=8,'vocab_1'=4] {'vocab_0'}, dimensions={0}, use_global_device_ids=true | all-gather | bytes 576 | tf_op jit(solution)/shard_map/all_gather | solution.py:24
  103.2 11.9 %all-gather.2 = s32[32,4,4]{2,1,0:T(4,128)S(1)} all-gather(s32[8,4,4]{2,1,0:T(4,128)S(1)} %all-gather.9), channel_id=4, replica_groups=mesh['dp_0'=4,'dp_1'=2,'vocab_0'=8,'vocab_1'=4] {'vocab_1'}, dimensions={0}, use_global_device_ids=true | all-gather | bytes 2560 | tf_op jit(solution)/shard_map/all_gather | solution.py:24
  115.0 0.2 copy.14
  115.2 1.9 all-gather.3
  117.1 0.3 copy.16
  117.3 0.2 sub.270
  117.5 0.2 select_reduce_fusion.1
  117.7 0.1 slice_add_fusion.11
  117.8 34.1 %all-gather.19.cloned.1.call-done = bf16[1024,8192]{1,0:T(8,128)(2,1)} async-done(((bf16[128,8192]{1,0:T(8,128)(2,1)}), bf16[1024,8192]{1,0:T(8,128)(2,1)}) %all-gather.19.cloned.1.call-update) | async-done | bytes 16777232 | tf_op jit(solution)/shard_map/all_gather | solution.py:103
  151.8 14.3 %fusion.61 = (f32[1024]{0:T(1024)S(1)}, f32[1024,501]{0,1:T(8,128)S(1)}) fusion(bf16[1024,8192]{1,0:T(8,128)(2,1)} %all-gather.19.cloned.1.call-done, bf16[8192,501]{0,1:T(8,128)(2,1)} %param.7), kind=kOutput, calls=%fused_computation.115 | convolution fusion | flops 8405897216 | bytes 27041792 | tf_op jit(solution)/shard_map/dot_general | solution.py:79
  166.2 0.5 exponential_reduce_fusion
  166.7 10.7 %all-gather.10 = f32[4,3,1024]{2,1,0:T(4,128)S(1)} all-gather(f32[1,3,1024]{2,1,0:T(4,128)S(1)} %maximum_bitcast_fusion), channel_id=6, replica_groups=mesh['dp_0'=4,'dp_1'=2,'vocab_0'=8,'vocab_1'=4] {'dp_0'}, dimensions={0}, use_global_device_ids=true | all-gather | bytes 61440 | tf_op jit(solution)/shard_map/all_gather | solution.py:50
  177.5 0.1 fusion.28
  177.6 1.8 all-gather.11
  179.5 26.3 %all-gather.12 = f32[8,3,1024]{2,1,0:T(4,128)S(1)} all-gather(f32[1,3,1024]{2,1,0:T(4,128)S(1)} %maximum_bitcast_fusion.2), channel_id=8, replica_groups=mesh['dp_0'=4,'dp_1'=2,'vocab_0'=8,'vocab_1'=4] {'vocab_0'}, dimensions={0}, use_global_device_ids=true | all-gather | bytes 110592 | tf_op jit(solution)/shard_map/all_gather | solution.py:50
  205.8 0.1 fusion.2
  205.9 12.2 %all-gather.13 = f32[4,3,1024]{2,1,0:T(4,128)S(1)} all-gather(f32[1,3,1024]{2,1,0:T(4,128)S(1)} %maximum_bitcast_fusion.3), channel_id=9, replica_groups=mesh['dp_0'=4,'dp_1'=2,'vocab_0'=8,'vocab_1'=4] {'vocab_1'}, dimensions={0}, use_global_device_ids=true | all-gather | bytes 61440 | tf_op jit(solution)/shard_map/all_gather | solution.py:50
  218.2 1.2 fusion.53
  219.5 0.1 select_reduce_fusion.2
  219.5 9.6 %all-reduce.3 = (f32[8]{0:T(128)S(1)}, f32[8]{0:T(128)S(1)}) all-reduce(f32[8]{0:T(128)S(1)} %get-tuple-element.6, f32[8]{0:T(128)S(1)} %get-tuple-element.5), channel_id=1, replica_groups=mesh['dp_0'=4,'dp_1'=2,'vocab_0'=8,'vocab_1'=4] {'dp_0'}, use_global_device_ids=true, to_apply=%region_5.6 | all-reduce | flops 16 | bytes 128 | tf_op jit(solution)/shard_map/psum | solution.py:75
  229.1 2.5 all-reduce.4
  231.5 15.9 %all-reduce.1 = (f32[8]{0:T(128)S(1)}, f32[8]{0:T(128)S(1)}) all-reduce(f32[8]{0:T(128)S(1)} %get-tuple-element.13, f32[8]{0:T(128)S(1)} %get-tuple-element.14), channel_id=1, replica_groups=mesh['dp_0'=4,'dp_1'=2,'vocab_0'=8,'vocab_1'=4] {'vocab_0'}, use_global_device_ids=true, to_apply=%region_7.8 | all-reduce | flops 16 | bytes 128 | tf_op jit(solution)/shard_map/psum | solution.py:75
  247.5 10.6 %all-reduce.2 = (f32[8]{0:T(128)}, f32[8]{0:T(128)}) all-reduce(f32[8]{0:T(128)S(1)} %get-tuple-element.7, f32[8]{0:T(128)S(1)} %get-tuple-element.8), channel_id=1, replica_groups=mesh['dp_0'=4,'dp_1'=2,'vocab_0'=8,'vocab_1'=4] {'vocab_1'}, use_global_device_ids=true, to_apply=%region_8.9 | all-reduce | flops 16 | bytes 128 | tf_op jit(solution)/shard_map/psum | solution.py:75
  (27 shorter events, 0.3 us)
Async XLA Ops:
  7.2 60.4 %copy-start.4 = (u32[256]{0:T(256)S(1)}, u32[256]{0:T(256)}, u32[]{:S(2)}) copy-start(u32[256]{0:T(256)} %constant.51) | copy-start | bytes 3076
  7.2 57.2 %copy-start = (s32[4]{0:T(128)S(1)}, s32[4]{0:T(128)}, u32[]{:S(2)}) copy-start(s32[4]{0:T(128)} %param.9) | copy-start | bytes 52
  7.2 61.7 %copy-start.3 = (s32[4]{0:T(128)S(1)}, s32[4]{0:T(128)}, u32[]{:S(2)}) copy-start(s32[4]{0:T(128)} %param.8) | copy-start | bytes 52
  7.2 110.3 %copy-start.1 = (s32[257]{0:T(512)S(1)}, s32[257]{0:T(512)}, u32[]{:S(2)}) copy-start(s32[257]{0:T(512)} %param.11) | copy-start | bytes 3088
  7.2 57.1 %all-gather.17.cloned.1.call-start = ((), (), s32[]{:S(2)}) async-start(), calls=%async_computation | async-start | bytes 2359296 | tf_op jit(solution)/shard_map/all_gather | solution.py:38
  21.0 130.8 %all-gather.19.cloned.1.call-start = ((), (), s32[]{:S(2)}) async-start(), calls=%async_computation.1 | async-start | bytes 18874368 | tf_op jit(solution)/shard_map/all_gather | solution.py:103
  64.4 153.8 %collective-permute-start = (s32[1]{0:T(128)}, s32[1]{0:T(128)}, u32[]{:S(2)}, u32[]{:S(2)}) collective-permute-start(s32[1]{0:T(128)} %add.335), channel_id=1, source_target_pairs={{1,0},{2,1},{3,2},{4,3},{5,4},{6,5},{7,6},{8,7},{9,8},{10,9},{11,1... | collective-permute-start | bytes 20 | tf_op jit(solution)/shard_map/ppermute | solution.py:71
  166.2 52.1 %copy-start.2 = (s32[4]{0:T(128)S(1)}, s32[4]{0:T(128)}, u32[]{:S(2)}) copy-start(s32[4]{0:T(128)} %param.10) | copy-start | bytes 52
Sparse Core Ops, SparseCore 0:
  21.1 43.1 all-gather.16
  66.2 85.6 all-gather.18
where the time goes:
time: 265 us
  blocking collectives  150 us (57%)
  waiting for transfers between devices  77.4 us (29%)
  between operations  14.9 us (6%)
  matrix products  14.3 us (5%)
  starting transfers between devices  3.28 us (1%)
    all_gather x4, blocking collectives, gathered_once(): both, at, found = (lax.all_gather(jnp.concatenate(lines), axis), 0, {})  51.1 us
    all_gather x1, waiting for transfers between devices, whole_of(): out = lax.all_gather(out, axes[number], axis=dim, tiled=True)  43.2 us
    all_gather x3, blocking collectives, gather_in_order(): pieces = lax.all_gather(pieces, axes[k])  39.7 us
    psum x4, blocking collectives, one_axis_at_a_time(): return functools.reduce(lax.psum, axes, value)  38.6 us
    all_gather x1, waiting for transfers between devices, body(): lax.all_gather(group_rows, DP, axis=0, tiled=True)  34.1 us
    dot_general x1, matrix products, shard_stats(): logits = jnp.dot(piece, lm_head, preferred_element_type=jnp.float32)  14.3 us
    all_gather x1, blocking collectives, whole_of(): out = lax.all_gather(out, axes[number], axis=dim, tiled=True)  13 us
    unnamed x1, blocking collectives  7.94 us
  transfers between devices with their start and end apart: 3, of which 2 were waited for; matrix products, arithmetic and copies ran while one was open for 6% of the time, Pallas kernels for 0%

commit v1 on v0

--- a/solution.py
+++ b/solution.py
@@ -100,7 +100,12 @@
     all_targets = gathered_by_axis(targets, DP_VOCAB, (0, 2, 3, 1), 0)
     per_piece = partial(shard_stats, lm_head=lm_head, all_targets=all_targets, col_start=col_start)
     group_rows = whole_of(hidden, VOCAB, 0)
-    stats = per_piece(lax.all_gather(group_rows, DP, axis=0, tiled=True), jnp.int32(0))
+    stats = per_piece(
+        jnp.concatenate(
+            lax.all_to_all(jnp.stack([group_rows] * lax.axis_size(DP)), DP, 0, 0), axis=0
+        ),
+        jnp.int32(0),
+    )
     top_all, total_all, picked_all = merged_by_axis(
         (stats[0], stats[1], stats[2]), DP_VOCAB, merge_rows
     )

time: 265 us -> 412 us (1.55)
  blocking collectives: 150 us -> 314 us
  waiting for transfers between devices: 77.4 us -> 43.3 us
  starting transfers between devices: 3.28 us -> 13.4 us
  local copies, waits for them, and re-layouts: 2.32 us -> 9.15 us
    unnamed x1, blocking collectives: 7.94 us -> 177 us
    all_gather x1 -> x0, waiting for transfers between devices: 34.1 us -> none  [body(): lax.all_gather(group_rows, DP, axis=0, tiled=True)]
    another operation x0 -> x1, local copies, waits for them, and re-layouts: none -> 6.84 us  [body(): jnp.stack([group_rows] * lax.axis_size(DP))]
    all_to_all x0 -> x1, starting transfers between devices: none -> 6.34 us  [body(): lax.all_to_all(jnp.stack([group_rows] * lax.axis_size(DP)), DP, 0, 0)]
    all_gather x3, blocking collectives: 39.7 us -> 35.4 us  [gather_in_order(): pieces = lax.all_gather(pieces, axes[k])]
  transfers between devices with their start and end apart: 3 -> 3, of which waited for: 2 -> 1; matrix products, arithmetic and copies ran while one was open for 6% -> 4% of each run, Pallas kernels for 0% -> 0%
where the time goes in v1:
time: 412 us
  blocking collectives  314 us (76%)
  waiting for transfers between devices  43.3 us (11%)
  between operations  14.9 us (4%)
  matrix products  14.3 us (3%)
  starting transfers between devices  13.4 us (3%)
  local copies, waits for them, and re-layouts  9.15 us (2%)
    unnamed x1, blocking collectives  177 us
    all_gather x4, blocking collectives, gathered_once(): both, at, found = (lax.all_gather(jnp.concatenate(lines), axis), 0, {})  49 us
    all_gather x1, waiting for transfers between devices, whole_of(): out = lax.all_gather(out, axes[number], axis=dim, tiled=True)  43.3 us
    psum x4, blocking collectives, one_axis_at_a_time(): return functools.reduce(lax.psum, axes, value)  39.5 us
    all_gather x3, blocking collectives, gather_in_order(): pieces = lax.all_gather(pieces, axes[k])  35.4 us
    dot_general x1, matrix products, shard_stats(): logits = jnp.dot(piece, lm_head, preferred_element_type=jnp.float32)  14.3 us
    all_gather x1, blocking collectives, whole_of(): out = lax.all_gather(out, axes[number], axis=dim, tiled=True)  13 us
  transfers between devices with their start and end apart: 3, of which 1 were waited for; matrix products, arithmetic and copies ran while one was open for 4% of the time, Pallas kernels for 0%

profile of v1, /device:TPU:2, one launch (start us, length us, event | category | flops | bytes accessed | tf_op | source)
XLA Modules:
  0.0 411.5 jit_solution(11447912467997019309)
XLA Ops:
  7.2 13.0 %all-gather.8 = bf16[4,4,8192]{2,1,0:T(4,128)(2,1)S(1)} all-gather(bf16[1,4,8192]{2,1,0:T(4,128)(2,1)} %bitcast.296), channel_id=1, replica_groups=mesh['dp_0'=4,'dp_1'=2,'vocab_0'=8,'vocab_1'=4] {'vocab_1'}, dimensions={0}, use_global_device_ids=true | all-gather | bytes 327680 | tf_op jit(solution)/shard_map/all_gather | solution.py:38
  20.2 0.8 reshape.926
  21.0 43.3 %all-gather.16.cloned.1.call-done = bf16[128,8192]{1,0:T(8,128)(2,1)} async-done(((bf16[16,8192]{1,0:T(8,128)(2,1)}), bf16[128,8192]{1,0:T(8,128)(2,1)}) %all-gather.16.cloned.1.call-update) | async-done | bytes 2097168 | tf_op jit(solution)/shard_map/all_gather | solution.py:38
  64.3 6.8 %stack.2 = bf16[8,128,8192]{2,1,0:T(8,128)(2,1)} broadcast(bf16[128,8192]{1,0:T(8,128)(2,1)} %all-gather.16.cloned.1.call-done), dimensions={1,2} | broadcast | bytes 18874368 | tf_op jit(solution)/shard_map/stack | solution.py:105
  71.1 6.3 %all-to-all-start = ((bf16[8,128,8192]{2,1,0:T(8,128)(2,1)}), bf16[8,128,8192]{2,1,0:T(8,128)(2,1)}, u32[]{:S(2)}, u32[]{:S(2)}) async-start(bf16[8,128,8192]{2,1,0:T(8,128)(2,1)} %stack.2), calls=%async_computation | async-start | bytes 33554432 | tf_op jit(solution)/shard_map/all_to_all | solution.py:105
  77.5 7.0 %collective-permute-start = (s32[1]{0:T(128)}, s32[1]{0:T(128)}, u32[]{:S(2)}, u32[]{:S(2)}) collective-permute-start(s32[1]{0:T(128)} %add.335), channel_id=1, source_target_pairs={{1,0},{2,1},{3,2},{4,3},{5,4},{6,5},{7,6},{8,7},{9,8},{10,9},{11,1... | collective-permute-start | bytes 20 | tf_op jit(solution)/shard_map/ppermute | solution.py:71
  84.5 0.6 dynamic-slice.1
  85.8 0.2 dynamic-update-slice
  86.0 177.1 %all-reduce = s32[16]{0:T(128)S(1)} all-reduce(s32[16]{0:T(128)S(1)} %dynamic-update-slice), channel_id=2, replica_groups=mesh['dp_0'=4,'dp_1'=2,'vocab_0'=8,'vocab_1'=4] {'dp_0'}, use_global_device_ids=true, to_apply=%add | all-reduce | flops 16 | bytes 128
  263.1 0.1 reshape.927
  263.1 21.4 %all-gather.9 = s32[8,4,4]{2,1,0:T(4,128)S(1)} all-gather(s32[1,4,4]{2,1,0:T(4,128)S(1)} %reshape.927), channel_id=3, replica_groups=mesh['dp_0'=4,'dp_1'=2,'vocab_0'=8,'vocab_1'=4] {'vocab_0'}, dimensions={0}, use_global_device_ids=true | all-gather | bytes 576 | tf_op jit(solution)/shard_map/all_gather | solution.py:24
  284.5 12.2 %all-gather.2 = s32[32,4,4]{2,1,0:T(4,128)S(1)} all-gather(s32[8,4,4]{2,1,0:T(4,128)S(1)} %all-gather.9), channel_id=4, replica_groups=mesh['dp_0'=4,'dp_1'=2,'vocab_0'=8,'vocab_1'=4] {'vocab_1'}, dimensions={0}, use_global_device_ids=true | all-gather | bytes 2560 | tf_op jit(solution)/shard_map/all_gather | solution.py:24
  296.7 0.2 copy.14
  296.9 1.9 all-gather.3
  298.8 0.3 copy.16
  299.0 0.2 sub.270
  299.2 0.2 select_reduce_fusion.1
  299.4 0.1 slice_add_fusion.11
  299.4 14.3 %fusion.61 = (f32[1024]{0:T(1024)S(1)}, f32[1024,501]{0,1:T(8,128)S(1)}) fusion(bf16[1024,8192]{1,0:T(8,128)(2,1)} %bitcast.1, bf16[8192,501]{0,1:T(8,128)(2,1)} %param.7), kind=kOutput, calls=%fused_computation.115 | convolution fusion | flops 8405897216 | bytes 27041792 | tf_op jit(solution)/shard_map/dot_general | solution.py:79
  313.8 0.5 exponential_reduce_fusion
  314.4 10.8 %all-gather.10 = f32[4,3,1024]{2,1,0:T(4,128)S(1)} all-gather(f32[1,3,1024]{2,1,0:T(4,128)S(1)} %maximum_bitcast_fusion), channel_id=6, replica_groups=mesh['dp_0'=4,'dp_1'=2,'vocab_0'=8,'vocab_1'=4] {'dp_0'}, dimensions={0}, use_global_device_ids=true | all-gather | bytes 61440 | tf_op jit(solution)/shard_map/all_gather | solution.py:50
  325.1 0.1 fusion.28
  325.2 1.8 all-gather.11
  327.1 24.6 %all-gather.12 = f32[8,3,1024]{2,1,0:T(4,128)S(1)} all-gather(f32[1,3,1024]{2,1,0:T(4,128)S(1)} %maximum_bitcast_fusion.2), channel_id=8, replica_groups=mesh['dp_0'=4,'dp_1'=2,'vocab_0'=8,'vocab_1'=4] {'vocab_0'}, dimensions={0}, use_global_device_ids=true | all-gather | bytes 110592 | tf_op jit(solution)/shard_map/all_gather | solution.py:50
  351.7 0.1 fusion.2
  351.9 11.9 %all-gather.13 = f32[4,3,1024]{2,1,0:T(4,128)S(1)} all-gather(f32[1,3,1024]{2,1,0:T(4,128)S(1)} %maximum_bitcast_fusion.3), channel_id=9, replica_groups=mesh['dp_0'=4,'dp_1'=2,'vocab_0'=8,'vocab_1'=4] {'vocab_1'}, dimensions={0}, use_global_device_ids=true | all-gather | bytes 61440 | tf_op jit(solution)/shard_map/all_gather | solution.py:50
  363.8 1.3 fusion.53
  365.1 0.1 select_reduce_fusion.2
  365.2 10.6 %all-reduce.3 = (f32[8]{0:T(128)S(1)}, f32[8]{0:T(128)S(1)}) all-reduce(f32[8]{0:T(128)S(1)} %get-tuple-element.6, f32[8]{0:T(128)S(1)} %get-tuple-element.5), channel_id=1, replica_groups=mesh['dp_0'=4,'dp_1'=2,'vocab_0'=8,'vocab_1'=4] {'dp_0'}, use_global_device_ids=true, to_apply=%region_5.6 | all-reduce | flops 16 | bytes 128 | tf_op jit(solution)/shard_map/psum | solution.py:75
  375.8 2.5 all-reduce.4
  378.2 15.8 %all-reduce.1 = (f32[8]{0:T(128)S(1)}, f32[8]{0:T(128)S(1)}) all-reduce(f32[8]{0:T(128)S(1)} %get-tuple-element.13, f32[8]{0:T(128)S(1)} %get-tuple-element.14), channel_id=1, replica_groups=mesh['dp_0'=4,'dp_1'=2,'vocab_0'=8,'vocab_1'=4] {'vocab_0'}, use_global_device_ids=true, to_apply=%region_7.8 | all-reduce | flops 16 | bytes 128 | tf_op jit(solution)/shard_map/psum | solution.py:75
  394.1 10.6 %all-reduce.2 = (f32[8]{0:T(128)}, f32[8]{0:T(128)}) all-reduce(f32[8]{0:T(128)S(1)} %get-tuple-element.7, f32[8]{0:T(128)S(1)} %get-tuple-element.8), channel_id=1, replica_groups=mesh['dp_0'=4,'dp_1'=2,'vocab_0'=8,'vocab_1'=4] {'vocab_1'}, use_global_device_ids=true, to_apply=%region_8.9 | all-reduce | flops 16 | bytes 128 | tf_op jit(solution)/shard_map/psum | solution.py:75
  (27 shorter events, 0.3 us)
Async XLA Ops:
  7.2 57.1 %all-gather.16.cloned.1.call-start = ((), (), s32[]{:S(2)}) async-start(), calls=%async_computation.1 | async-start | bytes 2359296 | tf_op jit(solution)/shard_map/all_gather | solution.py:38
  71.1 6.4 %copy-start = (s32[4]{0:T(128)S(1)}, s32[4]{0:T(128)}, u32[]{:S(2)}) copy-start(s32[4]{0:T(128)} %param.9) | copy-start | bytes 52
  71.1 13.4 %copy-start.4 = (u32[256]{0:T(256)S(1)}, u32[256]{0:T(256)}, u32[]{:S(2)}) copy-start(u32[256]{0:T(256)} %constant.51) | copy-start | bytes 3076
  71.1 14.6 %copy-start.3 = (s32[4]{0:T(128)S(1)}, s32[4]{0:T(128)}, u32[]{:S(2)}) copy-start(s32[4]{0:T(128)} %param.8) | copy-start | bytes 52
  71.1 228.1 %copy-start.1 = (s32[257]{0:T(512)S(1)}, s32[257]{0:T(512)}, u32[]{:S(2)}) copy-start(s32[257]{0:T(512)} %param.11) | copy-start | bytes 3088
  71.1 228.3 %all-to-all-start = ((bf16[8,128,8192]{2,1,0:T(8,128)(2,1)}), bf16[8,128,8192]{2,1,0:T(8,128)(2,1)}, u32[]{:S(2)}, u32[]{:S(2)}) async-start(bf16[8,128,8192]{2,1,0:T(8,128)(2,1)} %stack.2), calls=%async_computation | async-start | bytes 33554432 | tf_op jit(solution)/shard_map/all_to_all | solution.py:105
  77.5 286.3 %collective-permute-start = (s32[1]{0:T(128)}, s32[1]{0:T(128)}, u32[]{:S(2)}, u32[]{:S(2)}) collective-permute-start(s32[1]{0:T(128)} %add.335), channel_id=1, source_target_pairs={{1,0},{2,1},{3,2},{4,3},{5,4},{6,5},{7,6},{8,7},{9,8},{10,9},{11,1... | collective-permute-start | bytes 20 | tf_op jit(solution)/shard_map/ppermute | solution.py:71
  313.8 50.1 %copy-start.2 = (s32[4]{0:T(128)S(1)}, s32[4]{0:T(128)}, u32[]{:S(2)}) copy-start(s32[4]{0:T(128)} %param.10) | copy-start | bytes 52
Sparse Core Ops, SparseCore 0:
  21.1 43.1 all-gather.15
